TPU v7x, 128 devices: a whole 4x4x4 slice. The times are simulated.
128 devices in a mesh: dp: 16 (over y, x_lo, core), tensor: 8 (over z, x_hi).
Axes of the slice: x: 4 (x_hi: 2, x_lo: 2; x = x_hi * 2 + x_lo), y: 4, z: 4, core: 2. Of those that a mesh axis runs over, the one named last changes fastest.
Arguments:
- arrived: bfloat16 [256, 128, 1536], P(('dp', 'tensor')), may hold values from -6 to 6
- destination: int32 [256], replicated, may hold values from 0 to 15, as said below
- query_of: int32 [256], replicated, may hold values from 0 to 31, as said below
- lengths: int32 [256], replicated, may hold values from 32 to 128
- attn_gain: float32 [1536], replicated, may hold values from 0.25 to 1.75
- q_weight: bfloat16 [1536, 1024], P(None, 'tensor')
- q_bias: bfloat16 [1024], P('tensor'), may hold values from -3 to 3
- k_weight: bfloat16 [1536, 256], replicated
- v_weight: bfloat16 [1536, 256], replicated, may hold values from -0.15625 to 0.15625
- v_bias: bfloat16 [256], replicated, may hold values from -3 to 3
- o_weight: bfloat16 [1024, 1536], P('tensor'), may hold values from -0.1875 to 0.1875
- mlp_gain: float32 [1536], replicated, may hold values from 0.25 to 1.75
- w_gate: bfloat16 [1536, 8960], P(None, 'tensor'), may hold values from -0.15625 to 0.15625
- w_up: bfloat16 [1536, 8960], P(None, 'tensor'), may hold values from -0.15625 to 0.15625
- w_down: bfloat16 [8960, 1536], P('tensor'), may hold values from -0.0625 to 0.0625
- final_gain: float32 [1536], replicated, may hold values from 0.25 to 1.75
- score_weight: float32 [1536], replicated, may hold values from -0.15625 to 0.15625
Outputs:
- hidden_out: bfloat16 [128, 256, 1536], P('tensor', 'dp')
- centred: float32 [256], P('dp')
- query_mean: float32 [32], P('dp')
Inputs may be any that keep to these rules, and one draw needn't show every extreme that they name: In each aligned block of 16 pairs every destination occurs exactly once. `query_of`: each query has exactly 8 pairs.
All inputs are finite; a program needn't handle non-finite values.
Results may differ from a plain program's by a relative error of at most 0.02.
The roundings to bfloat16 on the way count: a program that leaves them out, or rounds other values in their place, can miss the bound.
Values may be sent and summed in bfloat16 or wider, within the bound.
A program may use at most 128 MiB of HBM per device.

v0:
```python
import math
import jax
import jax.numpy as jnp
from jax import lax
from jax.sharding import Mesh
from jax.sharding import PartitionSpec as P

KV_HEADS = 2
HEAD_DIM = 128
HEADS = 8
QUERY_DP = 2
TENSOR = ("tensor_0", "tensor_1")
DP_TENSOR = ("dp", "tensor_0", "tensor_1")
theta_base = 1000000.0
norm_eps = 1e-06


def gather_axes(x, axes, dim):
    for axis in reversed(axes):
        x = lax.all_gather(x, axis, axis=dim, tiled=True)
    return x


def copy_for_each(x, axis):
    copies = jnp.broadcast_to(x, (lax.axis_size(axis), *x.shape))
    return lax.all_to_all(copies, axis, split_axis=0, concat_axis=0, tiled=True)


def taken_together(x, axis):
    return copy_for_each(x, axis).sum(axis=0)


def rms_scale(values, gain_vector):
    floats = values.astype(jnp.float32)
    return (
        floats
        * lax.rsqrt(jnp.mean(floats * floats, axis=-1, keepdims=True) + norm_eps)
        * gain_vector
    )


def frequency_table(head_dim):
    return theta_base ** (-2.0 * jnp.arange(head_dim // 2, dtype=jnp.float32) / head_dim)


def rotate(values, cosine_table, sine_table):
    half_dim = values.shape[-1] // 2
    first_half = values[..., :half_dim]
    second_half = values[..., half_dim:]
    return jnp.concatenate(
        [
            first_half * cosine_table - second_half * sine_table,
            second_half * cosine_table + first_half * sine_table,
        ],
        axis=-1,
    )


def on_device(
    arrived,
    destination,
    query_of,
    lengths,
    attn_gain,
    q_weight,
    q_bias,
    k_weight,
    v_weight,
    v_bias,
    o_weight,
    mlp_gain,
    w_gate,
    w_up,
    w_down,
    final_gain,
    score_weight,
):
    group_index = lax.axis_index("dp")
    tensor_index = lax.axis_index(TENSOR)
    tensor_count = lax.axis_size(TENSOR)
    row_blocks = lax.all_to_all(arrived, TENSOR, split_axis=1, concat_axis=0, tiled=True)
    pairs_here = row_blocks.shape[0]
    row_targets = lax.dynamic_slice_in_dim(destination, group_index * pairs_here, pairs_here)
    local_order = jnp.argsort(row_targets * pairs_here + jnp.arange(pairs_here, dtype=jnp.int32))
    sorted_rows = jnp.transpose(jnp.take(row_blocks, local_order, axis=0), (1, 0, 2))
    resident = lax.all_to_all(sorted_rows, "dp", split_axis=1, concat_axis=1, tiled=True)
    total_pairs = destination.shape[0]
    global_order = jnp.argsort(destination * total_pairs + jnp.arange(total_pairs, dtype=jnp.int32))
    my_pairs = lax.dynamic_slice_in_dim(global_order, group_index * pairs_here, pairs_here)
    my_lengths = jnp.take(lengths, my_pairs)
    my_queries = jnp.take(query_of, my_pairs)
    seq_local = resident.shape[0]
    seq_len = seq_local * tensor_count
    heads_here = q_weight.shape[1] // HEAD_DIM
    kv_head = tensor_index * heads_here // (HEADS // KV_HEADS)
    key_cols = lax.dynamic_slice_in_dim(k_weight, kv_head * HEAD_DIM, HEAD_DIM, 1)
    value_cols = lax.dynamic_slice_in_dim(v_weight, kv_head * HEAD_DIM, HEAD_DIM, 1)
    value_shift = lax.dynamic_slice_in_dim(v_bias, kv_head * HEAD_DIM, HEAD_DIM)
    joint_weight = jnp.concatenate([q_weight, key_cols, value_cols], axis=1)
    joint_bias = jnp.concatenate(
        [
            q_bias.astype(jnp.float32),
            jnp.zeros((HEAD_DIM,), jnp.float32),
            value_shift.astype(jnp.float32),
        ]
    )
    frequencies = frequency_table(HEAD_DIM)
    query_width = heads_here * HEAD_DIM
    normed = rms_scale(resident, attn_gain).astype(jnp.bfloat16)
    piece_rows = lax.all_gather(normed, TENSOR, axis=0, tiled=True)
    row_total = piece_rows.shape[0]
    projected_rows = (
        jnp.einsum("spd,de->spe", piece_rows, joint_weight, preferred_element_type=jnp.float32)
        + joint_bias
    )
    angles = (
        jnp.arange(row_total, dtype=jnp.int32).astype(jnp.float32)[:, None] * frequencies[None, :]
    )
    cosine_table = jnp.cos(angles)[:, None, None, :]
    sine_table = jnp.sin(angles)[:, None, None, :]
    query_rows = projected_rows[..., :query_width].reshape(
        row_total, pairs_here, heads_here, HEAD_DIM
    )
    key_rows = projected_rows[..., query_width : query_width + HEAD_DIM].reshape(
        row_total, pairs_here, 1, HEAD_DIM
    )
    value_rows = projected_rows[..., query_width + HEAD_DIM :]
    query_rows = rotate(query_rows, cosine_table, sine_table).reshape(
        row_total, pairs_here, query_width
    )
    key_rows = rotate(key_rows, cosine_table, sine_table).reshape(row_total, pairs_here, HEAD_DIM)
    projected = jnp.concatenate([query_rows, key_rows, value_rows], axis=-1).astype(jnp.bfloat16)
    query_all = projected[..., :query_width].reshape(seq_len, pairs_here, heads_here, HEAD_DIM)
    key_all = projected[..., query_width : query_width + HEAD_DIM]
    value_all = projected[..., query_width + HEAD_DIM :]
    logits = jnp.einsum(
        "qphe,kpe->phqk", query_all, key_all, preferred_element_type=jnp.float32
    ) / math.sqrt(HEAD_DIM)
    positions = jnp.arange(seq_len, dtype=jnp.int32)
    allowed = (positions[None, :] <= positions[:, None])[None, :, :] & (
        positions[None, None, :] < my_lengths[:, None, None]
    )
    logits = jnp.where(allowed[:, None, :, :], logits, -1e30)
    shifted = jnp.exp(logits - jnp.max(logits, axis=-1, keepdims=True))
    probs = (shifted / jnp.sum(shifted, axis=-1, keepdims=True)).astype(jnp.bfloat16)
    context = jnp.einsum(
        "phqk,kpe->qphe", probs, value_all, preferred_element_type=jnp.float32
    ).astype(jnp.bfloat16)
    context = context.reshape(seq_len, pairs_here, query_width)
    own_context = lax.all_to_all(context, TENSOR, split_axis=0, concat_axis=2, tiled=True)
    attended = jnp.einsum(
        "spe,ed->spd",
        own_context,
        gather_axes(o_weight, TENSOR, 0),
        preferred_element_type=jnp.float32,
    )
    after_attention = (resident.astype(jnp.float32) + attended).astype(jnp.bfloat16)
    normed_mlp = rms_scale(after_attention, mlp_gain).astype(jnp.bfloat16)
    piece_rows = lax.all_gather(normed_mlp, TENSOR, axis=0, tiled=True)
    gate_values = jnp.einsum("spd,df->spf", piece_rows, w_gate, preferred_element_type=jnp.float32)
    up_values = jnp.einsum("spd,df->spf", piece_rows, w_up, preferred_element_type=jnp.float32)
    activated = (jax.nn.silu(gate_values) * up_values).astype(jnp.bfloat16)
    mlp_sum = lax.psum_scatter(
        jnp.einsum("spf,fd->spd", activated, w_down, preferred_element_type=jnp.float32).astype(
            jnp.bfloat16
        ),
        TENSOR,
        scatter_dimension=0,
        tiled=True,
    ).astype(jnp.float32)
    hidden_out = (after_attention.astype(jnp.float32) + mlp_sum).astype(jnp.bfloat16)
    local_positions = tensor_index * seq_local + jnp.arange(seq_local, dtype=jnp.int32)
    is_last = (local_positions[:, None] == (my_lengths - 1)[None, :]).astype(jnp.bfloat16)
    last_rows = jnp.einsum("sp,spd->pd", is_last, hidden_out, preferred_element_type=jnp.float32)
    partial_score = jnp.sum(rms_scale(last_rows, final_gain) * score_weight, axis=-1)
    pair_score = taken_together(partial_score, TENSOR)
    query_total = lax.axis_size("dp") * QUERY_DP
    membership = (my_queries[:, None] == jnp.arange(query_total, dtype=jnp.int32)[None, :]).astype(
        jnp.float32
    )
    totals = taken_together(jnp.dot(pair_score, membership), "dp")
    mean_all = totals / (total_pairs // query_total)
    centred = pair_score - jnp.dot(membership, mean_all)
    query_mean = lax.dynamic_slice_in_dim(mean_all, group_index * QUERY_DP, QUERY_DP)
    return (hidden_out, centred, query_mean)


def solution(mesh):
    split = Mesh(mesh.devices.reshape(mesh.shape["dp"], 4, 2), ("dp", "tensor_0", "tensor_1"))
    placed = (
        P(DP_TENSOR, None, None),
        P(),
        P(),
        P(),
        P(),
        P(None, TENSOR),
        P(TENSOR),
        P(),
        P(),
        P(),
        P(TENSOR, None),
        P(),
        P(None, TENSOR),
        P(None, TENSOR),
        P(TENSOR, None),
        P(),
        P(),
    )
    return jax.shard_map(
        on_device,
        mesh=split,
        in_specs=placed,
        out_specs=(P(TENSOR, "dp", None), P("dp"), P("dp")),
        check_vma=False,
    )
```

profile of v0, /device:TPU:1, one launch (start us, length us, event | category | flops | bytes accessed | tf_op | source)
XLA Modules:
  0.0 443.9 jit_solution(2030019210064797637)
XLA Ops:
  7.2 3.0 copy.56
  10.2 8.3 %all-to-all-start = ((bf16[2,128,1536]{2,0,1:T(2,128)(2,1)}), bf16[2,128,1536]{2,0,1:T(2,128)(2,1)}, u32[]{:S(2)}, u32[]{:S(2)}) async-start(bf16[2,128,1536]{2,0,1:T(2,128)(2,1)} %copy.56), calls=%async_computation | async-start | bytes 1572864 | tf_op jit(solution)/shard_map/all_to_all | solution.py:81
  19.3 1.2 sort.34
  21.2 3.2 sort.35
  24.5 7.3 %all-to-all-done = bf16[2,128,1536]{2,0,1:T(2,128)(2,1)} async-done(((bf16[2,128,1536]{2,0,1:T(2,128)(2,1)}), bf16[2,128,1536]{2,0,1:T(2,128)(2,1)}, u32[]{:S(2)}, u32[]{:S(2)}) %all-to-all-start) | async-done | bytes 786464 | tf_op jit(solution)/shard_map/all_to_all | solution.py:81
  31.8 1.2 copy.57
  34.0 2.6 gather_fusion
  36.6 1.3 select_bitcast_fusion
  37.9 19.4 %all_to_all.53 = bf16[16,16,1536]{2,0,1:T(8,128)(2,1)S(1)} all-to-all(bf16[16,16,1536]{2,0,1:T(8,128)(2,1)S(1)} %select_bitcast_fusion), channel_id=1, replica_groups=mesh['dp'=16,'tensor_0'=4,'tensor_1'=2] {'dp'}, dimensions={1} | all-to-all | bytes 1572864 | tf_op jit(solution)/shard_map/all_to_all | solution.py:86
  58.1 1.1 fusion.17
  59.3 13.9 %all_gather.13 = bf16[256,1536]{1,0:T(8,128)(2,1)} all-gather(bf16[128,1536]{1,0:T(8,128)(2,1)} %param.29), channel_id=1, replica_groups=mesh['dp'=16,'tensor_0'=4,'tensor_1'=2] {'tensor_1'}, dimensions={0}, use_global_device_ids=true | all-gather | bytes 1179648 | tf_op jit(solution)/shard_map/all_gather | solution.py:20
  75.9 2.1 constant_dynamic-slice_fusion
  77.9 66.0 %all-gather.4.cloned.1.call-done = bf16[128,16,1536]{2,0,1:T(8,128)(2,1)} async-done(((bf16[16,16,1536]{2,0,1:T(8,128)(2,1)}), bf16[128,16,1536]{2,0,1:T(8,128)(2,1)}) %all-gather.4.cloned.1.call-update) | async-done | bytes 6291472 | tf_op jit(solution)/shard_map/all_gather | solution.py:110
  144.0 5.9 %convolution_add_fusion = f32[128,16,384]{2,0,1:T(8,128)S(1)} fusion(bf16[128,16,1536]{2,0,1:T(8,128)(2,1)} %all-gather.4.cloned.1.call-done, f32[384]{0:T(512)S(1)} %pad_maximum_fusion, bf16[1536,128]{1,0:T(8,128)(2,1)} %get-tuple-element.45, bf16[1536,128]{1,0:T(8,128)(2,1)} %get-tuple-element.46, bf16[1536,128]{1,0:T(8,128)(2,1)} %param.24), kind=kOutput, calls=%fused_computation.16 | convolution fusion | flops 2420244480 | bytes 10618368 | tf_op jit(solution)/shard_map/spd,de->spe/dot_general | solution.py:113
  152.5 1.2 fusion.20
  153.7 2.3 copy.61
  156.0 15.4 %all_to_all.54 = bf16[128,16,128]{2,1,0:T(8,128)(2,1)S(1)} all-to-all(bf16[128,16,128]{2,1,0:T(8,128)(2,1)} %copy.61), channel_id=1, replica_groups=mesh['dp'=16,'tensor_0'=4,'tensor_1'=2] {'tensor_0','tensor_1'}, dimensions={0} | all-to-all | bytes 1048576 | tf_op jit(solution)/shard_map/all_to_all | solution.py:150
  171.5 1.1 copy.73
  172.6 2.1 reshape.241
  174.7 14.6 %all-gather.6.cloned.1.call-done = bf16[1024,1536]{1,0:T(8,128)(2,1)} async-done(((bf16[256,1536]{1,0:T(8,128)(2,1)}), bf16[1024,1536]{1,0:T(8,128)(2,1)}) %all-gather.6.cloned.1.call-update) | async-done | bytes 3145744 | tf_op jit(solution)/shard_map/all_gather | solution.py:20
  189.3 3.3 multiply_reduce_fusion
  192.6 1.1 copy-done.5
  195.1 88.1 %all-gather.8.cloned.1.call-done = bf16[128,16,1536]{2,0,1:T(8,128)(2,1)} async-done(((bf16[16,16,1536]{2,0,1:T(8,128)(2,1)}), bf16[128,16,1536]{2,0,1:T(8,128)(2,1)}) %all-gather.8.cloned.1.call-update) | async-done | bytes 6291472 | tf_op jit(solution)/shard_map/all_gather | solution.py:159
  283.2 10.6 %fusion.1 = f32[128,16,1120]{0,2,1:T(8,128)S(1)} fusion(bf16[128,16,1536]{2,0,1:T(8,128)(2,1)} %all-gather.8.cloned.1.call-done, bf16[1536,1120]{0,1:T(8,128)(2,1)} %param.32), kind=kOutput, calls=%fused_computation.6 | convolution fusion | flops 7046430720 | bytes 18907136 | tf_op jit(solution)/shard_map/spd,df->spf/dot_general | solution.py:161
  293.9 8.7 %multiply_convert_fusion = bf16[128,16,1120]{0,2,1:T(8,128)(2,1)S(1)} fusion(f32[128,16,1120]{0,2,1:T(8,128)S(1)} %fusion.1, bf16[128,16,1536]{2,0,1:T(8,128)(2,1)S(1)} %copy-done.11, bf16[1536,1120]{0,1:T(8,128)(2,1)S(1)} %copy-done.12), kind=kOutput, calls=%fused_computation.3 | convolution fusion | flops 7060193280 | bytes 23494656 | tf_op jit(solution)/shard_map/spd,df->spf/dot_general | solution.py:160
  302.6 10.3 %convolution_convert_fusion = bf16[128,16,1536]{2,0,1:T(8,128)(2,1)} fusion(bf16[128,16,1120]{0,2,1:T(8,128)(2,1)S(1)} %multiply_convert_fusion, bf16[1120,1536]{1,0:T(8,128)(2,1)S(1)} %copy-done), kind=kOutput, calls=%fused_computation.4 | convolution fusion | flops 7049576448 | bytes 14319616 | tf_op jit(solution)/shard_map/spf,fd->spd/dot_general | solution.py:164
  313.1 95.8 %reduce-scatter.2.cloned.1.call-done = bf16[16,16,1536]{2,0,1:T(8,128)(2,1)} async-done(((bf16[128,16,1536]{2,0,1:T(8,128)(2,1)}), bf16[16,16,1536]{2,0,1:T(8,128)(2,1)}) %reduce-scatter.2.cloned.1.call-update) | async-done | bytes 786448 | tf_op jit(solution)/shard_map/reduce_scatter | solution.py:163
  408.9 1.8 add_convert_fusion
  412.2 8.9 %all_to_all.55 = f32[8,1,16]{2,1,0:T(1,128)S(1)} all-to-all(f32[8,1,16]{2,1,0:T(1,128)S(1)} %broadcast_in_dim.30), channel_id=1, replica_groups=mesh['dp'=16,'tensor_0'=4,'tensor_1'=2] {'tensor_0','tensor_1'}, dimensions={0} | all-to-all | bytes 1024 | tf_op jit(solution)/shard_map/all_to_all | solution.py:26
  421.9 8.7 %all-to-all-start.4 = ((f32[16,1,32]{2,1,0:T(1,128)}), f32[16,1,32]{2,1,0:T(1,128)S(1)}, u32[]{:S(2)}, u32[]{:S(2)}) async-start(f32[16,1,32]{2,1,0:T(1,128)} %broadcast_in_dim.31), calls=%async_computation.5 | async-start | bytes 16384 | tf_op jit(solution)/shard_map/all_to_all | solution.py:26
  430.6 2.4 copy.66
  433.0 3.1 all-to-all-done.4
  (81 shorter events, 13.7 us)
Async XLA Ops:
  7.2 295.4 %copy-start = (bf16[1120,1536]{1,0:T(8,128)(2,1)S(1)}, bf16[1120,1536]{1,0:T(8,128)(2,1)}, u32[]{:S(2)}) copy-start(bf16[1120,1536]{1,0:T(8,128)(2,1)} %param.33) | copy-start | bytes 10321924
  10.2 21.7 %all-to-all-start = ((bf16[2,128,1536]{2,0,1:T(2,128)(2,1)}), bf16[2,128,1536]{2,0,1:T(2,128)(2,1)}, u32[]{:S(2)}, u32[]{:S(2)}) async-start(bf16[2,128,1536]{2,0,1:T(2,128)(2,1)} %copy.56), calls=%async_computation | async-start | bytes 1572864 | tf_op jit(solution)/shard_map/all_to_all | solution.py:81
  18.5 125.5 %all-gather.4.cloned.1.call-start = ((), (), s32[]{:S(2)}) async-start(), calls=%async_computation.6 | async-start | bytes 7077888 | tf_op jit(solution)/shard_map/all_gather | solution.py:110
  33.0 25.1 %copy-start.7 = (f32[1536]{0:T(1024)S(1)}, f32[1536]{0:T(1024)}, u32[]{:S(2)}) copy-start(f32[1536]{0:T(1024)} %param.23) | copy-start | bytes 18436
  37.9 35.5 %copy-start.13 = (bf16[128]{0:T(256)(128)(2,1)S(1)}, bf16[128]{0:T(256)(128)(2,1)}, u32[]{:S(2)}) copy-start(bf16[128]{0:T(256)(128)(2,1)} %param.25) | copy-start | bytes 772
  37.9 35.5 %copy-start.1 = (s32[256]{0:T(256)S(1)}, s32[256]{0:T(256)}, u32[]{:S(2)}) copy-start(s32[256]{0:T(256)} %param.22) | copy-start | bytes 3076
  37.9 36.2 %copy-start.2 = (s32[256]{0:T(256)S(1)}, s32[256]{0:T(256)}, u32[]{:S(2)}) copy-start(s32[256]{0:T(256)} %param.21) | copy-start | bytes 3076
  57.2 0.9 copy-start.3
  57.2 17.5 %copy-start.14 = (bf16[256]{0:T(256)(128)(2,1)S(1)}, bf16[256]{0:T(256)(128)(2,1)}, u32[]{:S(2)}) copy-start(bf16[256]{0:T(256)(128)(2,1)} %param.28) | copy-start | bytes 1540
  59.3 130.0 %all-gather.6.cloned.1.call-start = ((), (), s32[]{:S(2)}) async-start(), calls=%async_computation.7 | async-start | bytes 3932160 | tf_op jit(solution)/shard_map/all_gather | solution.py:20
  73.3 210.0 %all-gather.8.cloned.1.call-start = ((), (), s32[]{:S(2)}) async-start(), calls=%async_computation.8 | async-start | bytes 7077888 | tf_op jit(solution)/shard_map/all_gather | solution.py:159
  149.8 0.8 copy-start.6
  172.6 21.2 %copy-start.8 = (f32[1536]{0:T(1024)S(1)}, f32[1536]{0:T(1024)}, u32[]{:S(2)}) copy-start(f32[1536]{0:T(1024)} %param.30) | copy-start | bytes 18436
  192.6 1.1 copy-start.5
  194.9 214.0 %reduce-scatter.2.cloned.1.call-start = ((), (), s32[]{:S(2)}) async-start(), calls=%async_computation.9 | async-start | bytes 7077888 | tf_op jit(solution)/shard_map/reduce_scatter | solution.py:163
  283.2 10.6 %copy-start.11 = (bf16[128,16,1536]{2,0,1:T(8,128)(2,1)S(1)}, bf16[128,16,1536]{2,0,1:T(8,128)(2,1)}, u32[]{:S(2)}) copy-start(bf16[128,16,1536]{2,0,1:T(8,128)(2,1)} %all-gather.8.cloned.1.call-done) | copy-start | bytes 18874372
  283.2 10.6 %copy-start.12 = (bf16[1536,1120]{0,1:T(8,128)(2,1)S(1)}, bf16[1536,1120]{0,1:T(8,128)(2,1)}, u32[]{:S(2)}) copy-start(bf16[1536,1120]{0,1:T(8,128)(2,1)} %param.31) | copy-start | bytes 10321924
  312.9 99.1 %copy-start.9 = (f32[1536]{0:T(1024)S(1)}, f32[1536]{0:T(1024)}, u32[]{:S(2)}) copy-start(f32[1536]{0:T(1024)} %param.35) | copy-start | bytes 18436
  312.9 99.1 %copy-start.10 = (f32[1536]{0:T(1024)S(1)}, f32[1536]{0:T(1024)}, u32[]{:S(2)}) copy-start(f32[1536]{0:T(1024)} %param.34) | copy-start | bytes 18436
  410.7 0.9 copy-start.4
  421.9 14.2 %all-to-all-start.4 = ((f32[16,1,32]{2,1,0:T(1,128)}), f32[16,1,32]{2,1,0:T(1,128)S(1)}, u32[]{:S(2)}, u32[]{:S(2)}) async-start(f32[16,1,32]{2,1,0:T(1,128)} %broadcast_in_dim.31), calls=%async_computation.5 | async-start | bytes 16384 | tf_op jit(solution)/shard_map/all_to_all | solution.py:26
Sparse Core Ops, SparseCore 0:
  59.4 84.5 all-gather.3
  145.6 43.6 all-gather.5
  195.0 88.1 all-gather.7
  313.0 95.8 reduce-scatter.1
where the time goes:
time: 445 us; the launch traced here: 444 us
  waiting for transfers between devices  275 us (62%)
  blocking collectives  57.6 us (13%)
  matrix products  42 us (9%)
  local copies, waits for them, and re-layouts  23.9 us (5%)
  starting transfers between devices  17.3 us (4%)
  between operations  14.1 us (3%)
  other arithmetic  14 us (3%)
    reduce_scatter x1, waiting for transfers between devices, on_device(): lax.psum_scatter(jnp.einsum('spf,fd->spd', activated, w_down, preferred_e...  95.8 us
    all_gather x1, waiting for transfers between devices, on_device(): piece_rows = lax.all_gather(normed_mlp, TENSOR, axis=0, tiled=True)  88.1 us
    all_gather x1, waiting for transfers between devices, on_device(): piece_rows = lax.all_gather(normed, TENSOR, axis=0, tiled=True)  66 us
    all_to_all x1, blocking collectives, on_device(): lax.all_to_all(sorted_rows, 'dp', split_axis=1, concat_axis=1, tiled=True)  19.4 us
    all_to_all x1, blocking collectives, on_device(): lax.all_to_all(context, TENSOR, split_axis=0, concat_axis=2, tiled=True)  15.4 us
    all_gather x1, waiting for transfers between devices, gather_axes(): x = lax.all_gather(x, axis, axis=dim, tiled=True)  14.6 us
    all_gather x1, blocking collectives, gather_axes(): x = lax.all_gather(x, axis, axis=dim, tiled=True)  13.9 us
    dot_general x1, matrix products, on_device(): jnp.einsum('spd,df->spf', piece_rows, w_up, preferred_element_type=jnp.fl...  10.6 us
  transfers between devices with their start and end apart: 6, of which 6 were waited for; matrix products, arithmetic and copies ran while one was open for 6% of the time, Pallas kernels for 0%

commit v1 on v0

--- a/solution.py
+++ b/solution.py
@@ -156,7 +156,9 @@
     )
     after_attention = (resident.astype(jnp.float32) + attended).astype(jnp.bfloat16)
     normed_mlp = rms_scale(after_attention, mlp_gain).astype(jnp.bfloat16)
-    piece_rows = lax.all_gather(normed_mlp, TENSOR, axis=0, tiled=True)
+    piece_rows = jnp.concatenate(
+        lax.all_to_all(jnp.stack([normed_mlp] * lax.axis_size(TENSOR)), TENSOR, 0, 0), axis=0
+    )
     gate_values = jnp.einsum("spd,df->spf", piece_rows, w_gate, preferred_element_type=jnp.float32)
     up_values = jnp.einsum("spd,df->spf", piece_rows, w_up, preferred_element_type=jnp.float32)
     activated = (jax.nn.silu(gate_values) * up_values).astype(jnp.bfloat16)

time: 445 us -> 434 us (0.975)
  waiting for transfers between devices: 275 us -> 187 us
  blocking collectives: 57.6 us -> 135 us
    all_gather x1 -> x0, waiting for transfers between devices: 88.1 us -> none  [on_device(): piece_rows = lax.all_gather(normed_mlp, TENSOR, axis=0, tiled=True)]
    all_to_all x0 -> x1, blocking collectives: none -> 77.5 us  [on_device(): lax.all_to_all(jnp.stack([normed_mlp] * lax.axis_size(TENSOR)), TENSOR, 0...]
  transfers between devices with their start and end apart: 6 -> 5, of which waited for: 6 -> 5; matrix products, arithmetic and copies ran while one was open for 6% -> 6% of each run, Pallas kernels for 0% -> 0%
where the time goes in v1:
time: 434 us; the launch traced here: 433 us
  waiting for transfers between devices  187 us (43%)
  blocking collectives  135 us (31%)
  matrix products  40.8 us (9%)
  local copies, waits for them, and re-layouts  25.3 us (6%)
  starting transfers between devices  17.2 us (4%)
  between operations  14.1 us (3%)
  other arithmetic  13.1 us (3%)
    reduce_scatter x1, waiting for transfers between devices, on_device(): lax.psum_scatter(jnp.einsum('spf,fd->spd', activated, w_down, preferred_e...  96.3 us
    all_to_all x1, blocking collectives, on_device(): lax.all_to_all(jnp.stack([normed_mlp] * lax.axis_size(TENSOR)), TENSOR, 0...  77.5 us
    all_gather x1, waiting for transfers between devices, on_device(): piece_rows = lax.all_gather(normed, TENSOR, axis=0, tiled=True)  66 us
    all_to_all x1, blocking collectives, on_device(): lax.all_to_all(sorted_rows, 'dp', split_axis=1, concat_axis=1, tiled=True)  19.4 us
    all_to_all x1, blocking collectives, on_device(): lax.all_to_all(context, TENSOR, split_axis=0, concat_axis=2, tiled=True)  15.4 us
    all_gather x1, waiting for transfers between devices, gather_axes(): x = lax.all_gather(x, axis, axis=dim, tiled=True)  14.6 us
    all_gather x1, blocking collectives, gather_axes(): x = lax.all_gather(x, axis, axis=dim, tiled=True)  13.9 us
    dot_general x1, matrix products, on_device(): jnp.einsum('spf,fd->spd', activated, w_down, preferred_element_type=jnp.f...  10.3 us
  transfers between devices with their start and end apart: 5, of which 5 were waited for; matrix products, arithmetic and copies ran while one was open for 6% of the time, Pallas kernels for 0%

profile of v1, /device:TPU:1, one launch (start us, length us, event | category | flops | bytes accessed | tf_op | source)
XLA Modules:
  0.0 433.0 jit_solution(16589497834801438303)
XLA Ops:
  7.2 3.0 copy.58
  10.2 8.3 %all-to-all-start = ((bf16[2,128,1536]{2,0,1:T(2,128)(2,1)}), bf16[2,128,1536]{2,0,1:T(2,128)(2,1)}, u32[]{:S(2)}, u32[]{:S(2)}) async-start(bf16[2,128,1536]{2,0,1:T(2,128)(2,1)} %copy.58), calls=%async_computation | async-start | bytes 1572864 | tf_op jit(solution)/shard_map/all_to_all | solution.py:81
  19.3 1.2 sort.34
  21.2 3.2 sort.35
  24.5 7.3 %all-to-all-done = bf16[2,128,1536]{2,0,1:T(2,128)(2,1)} async-done(((bf16[2,128,1536]{2,0,1:T(2,128)(2,1)}), bf16[2,128,1536]{2,0,1:T(2,128)(2,1)}, u32[]{:S(2)}, u32[]{:S(2)}) %all-to-all-start) | async-done | bytes 786464 | tf_op jit(solution)/shard_map/all_to_all | solution.py:81
  31.8 1.2 copy.59
  34.0 2.6 gather_fusion
  36.6 1.3 select_bitcast_fusion
  37.9 19.4 %all_to_all.58 = bf16[16,16,1536]{2,0,1:T(8,128)(2,1)S(1)} all-to-all(bf16[16,16,1536]{2,0,1:T(8,128)(2,1)S(1)} %select_bitcast_fusion), channel_id=1, replica_groups=mesh['dp'=16,'tensor_0'=4,'tensor_1'=2] {'dp'}, dimensions={1} | all-to-all | bytes 1572864 | tf_op jit(solution)/shard_map/all_to_all | solution.py:86
  58.1 1.1 fusion.17
  59.3 13.9 %all_gather.10 = bf16[256,1536]{1,0:T(8,128)(2,1)} all-gather(bf16[128,1536]{1,0:T(8,128)(2,1)} %param.29), channel_id=1, replica_groups=mesh['dp'=16,'tensor_0'=4,'tensor_1'=2] {'tensor_1'}, dimensions={0}, use_global_device_ids=true | all-gather | bytes 1179648 | tf_op jit(solution)/shard_map/all_gather | solution.py:20
  75.9 2.1 constant_dynamic-slice_fusion
  77.9 66.0 %all-gather.3.cloned.1.call-done = bf16[128,16,1536]{2,0,1:T(8,128)(2,1)} async-done(((bf16[16,16,1536]{2,0,1:T(8,128)(2,1)}), bf16[128,16,1536]{2,0,1:T(8,128)(2,1)}) %all-gather.3.cloned.1.call-update) | async-done | bytes 6291472 | tf_op jit(solution)/shard_map/all_gather | solution.py:110
  144.0 5.9 %convolution_add_fusion = f32[128,16,384]{2,0,1:T(8,128)S(1)} fusion(bf16[128,16,1536]{2,0,1:T(8,128)(2,1)} %all-gather.3.cloned.1.call-done, f32[384]{0:T(512)S(1)} %pad_maximum_fusion, bf16[1536,128]{1,0:T(8,128)(2,1)} %get-tuple-element.45, bf16[1536,128]{1,0:T(8,128)(2,1)} %get-tuple-element.46, bf16[1536,128]{1,0:T(8,128)(2,1)} %param.24), kind=kOutput, calls=%fused_computation.16 | convolution fusion | flops 2420244480 | bytes 10618368 | tf_op jit(solution)/shard_map/spd,de->spe/dot_general | solution.py:113
  152.5 1.2 fusion.20
  153.7 2.3 copy.63
  156.0 15.4 %all_to_all.59 = bf16[128,16,128]{2,1,0:T(8,128)(2,1)S(1)} all-to-all(bf16[128,16,128]{2,1,0:T(8,128)(2,1)} %copy.63), channel_id=1, replica_groups=mesh['dp'=16,'tensor_0'=4,'tensor_1'=2] {'tensor_0','tensor_1'}, dimensions={0} | all-to-all | bytes 1048576 | tf_op jit(solution)/shard_map/all_to_all | solution.py:150
  171.5 1.1 copy.76
  172.6 2.1 reshape.247
  174.7 14.6 %all-gather.5.cloned.1.call-done = bf16[1024,1536]{1,0:T(8,128)(2,1)} async-done(((bf16[256,1536]{1,0:T(8,128)(2,1)}), bf16[1024,1536]{1,0:T(8,128)(2,1)}) %all-gather.5.cloned.1.call-update) | async-done | bytes 3145744 | tf_op jit(solution)/shard_map/all_gather | solution.py:20
  189.3 3.3 multiply_reduce_fusion
  192.6 1.1 copy-done.5
  194.7 77.5 %all_to_all.60 = bf16[8,16,16,1536]{3,1,2,0:T(8,128)(2,1)S(1)} all-to-all(bf16[8,16,16,1536]{3,1,2,0:T(8,128)(2,1)S(1)} %stack.2), channel_id=1, replica_groups=mesh['dp'=16,'tensor_0'=4,'tensor_1'=2] {'tensor_0','tensor_1'}, dimensions={0} | all-to-all | bytes 12582912 | tf_op jit(solution)/shard_map/all_to_all | solution.py:160
  272.9 9.5 %fusion.1 = f32[128,16,1120]{0,2,1:T(8,128)S(1)} fusion(bf16[128,16,1536]{2,0,1:T(8,128)(2,1)S(1)} %bitcast.109, bf16[1536,1120]{0,1:T(8,128)(2,1)} %param.32), kind=kOutput, calls=%fused_computation.6 | convolution fusion | flops 7046430720 | bytes 18907136 | tf_op jit(solution)/shard_map/spd,df->spf/dot_general | solution.py:163
  282.3 8.7 %multiply_convert_fusion = bf16[128,16,1120]{0,2,1:T(8,128)(2,1)S(1)} fusion(f32[128,16,1120]{0,2,1:T(8,128)S(1)} %fusion.1, bf16[128,16,1536]{2,0,1:T(8,128)(2,1)S(1)} %bitcast.110, bf16[1536,1120]{0,1:T(8,128)(2,1)S(1)} %copy-done.11), kind=kOutput, calls=%fused_computation.3 | convolution fusion | flops 7060193280 | bytes 23494656 | tf_op jit(solution)/shard_map/spd,df->spf/dot_general | solution.py:162
  291.1 10.3 %convolution_convert_fusion = bf16[128,16,1536]{2,0,1:T(8,128)(2,1)} fusion(bf16[128,16,1120]{0,2,1:T(8,128)(2,1)S(1)} %multiply_convert_fusion, bf16[1120,1536]{1,0:T(8,128)(2,1)S(1)} %copy-done), kind=kOutput, calls=%fused_computation.4 | convolution fusion | flops 7049576448 | bytes 14319616 | tf_op jit(solution)/shard_map/spf,fd->spd/dot_general | solution.py:166
  301.6 96.3 %reduce-scatter.2.cloned.1.call-done = bf16[16,16,1536]{2,0,1:T(8,128)(2,1)} async-done(((bf16[128,16,1536]{2,0,1:T(8,128)(2,1)}), bf16[16,16,1536]{2,0,1:T(8,128)(2,1)}) %reduce-scatter.2.cloned.1.call-update) | async-done | bytes 786448 | tf_op jit(solution)/shard_map/reduce_scatter | solution.py:165
  397.9 1.8 add_convert_fusion
  401.2 8.9 %all_to_all.61 = f32[8,1,16]{2,1,0:T(1,128)S(1)} all-to-all(f32[8,1,16]{2,1,0:T(1,128)S(1)} %broadcast_in_dim.30), channel_id=1, replica_groups=mesh['dp'=16,'tensor_0'=4,'tensor_1'=2] {'tensor_0','tensor_1'}, dimensions={0} | all-to-all | bytes 1024 | tf_op jit(solution)/shard_map/all_to_all | solution.py:26
  410.9 8.7 %all-to-all-start.5 = ((f32[16,1,32]{2,1,0:T(1,128)}), f32[16,1,32]{2,1,0:T(1,128)S(1)}, u32[]{:S(2)}, u32[]{:S(2)}) async-start(f32[16,1,32]{2,1,0:T(1,128)} %broadcast_in_dim.31), calls=%async_computation.6 | async-start | bytes 16384 | tf_op jit(solution)/shard_map/all_to_all | solution.py:26
  419.7 2.4 copy.69
  422.1 3.1 all-to-all-done.5
  (79 shorter events, 14.0 us)
Async XLA Ops:
  7.2 283.9 %copy-start = (bf16[1120,1536]{1,0:T(8,128)(2,1)S(1)}, bf16[1120,1536]{1,0:T(8,128)(2,1)}, u32[]{:S(2)}) copy-start(bf16[1120,1536]{1,0:T(8,128)(2,1)} %param.33) | copy-start | bytes 10321924
  10.2 21.7 %all-to-all-start = ((bf16[2,128,1536]{2,0,1:T(2,128)(2,1)}), bf16[2,128,1536]{2,0,1:T(2,128)(2,1)}, u32[]{:S(2)}, u32[]{:S(2)}) async-start(bf16[2,128,1536]{2,0,1:T(2,128)(2,1)} %copy.58), calls=%async_computation | async-start | bytes 1572864 | tf_op jit(solution)/shard_map/all_to_all | solution.py:81
  18.5 125.5 %all-gather.3.cloned.1.call-start = ((), (), s32[]{:S(2)}) async-start(), calls=%async_computation.7 | async-start | bytes 7077888 | tf_op jit(solution)/shard_map/all_gather | solution.py:110
  33.0 25.1 %copy-start.7 = (f32[1536]{0:T(1024)S(1)}, f32[1536]{0:T(1024)}, u32[]{:S(2)}) copy-start(f32[1536]{0:T(1024)} %param.23) | copy-start | bytes 18436
  37.9 35.5 %copy-start.12 = (bf16[128]{0:T(256)(128)(2,1)S(1)}, bf16[128]{0:T(256)(128)(2,1)}, u32[]{:S(2)}) copy-start(bf16[128]{0:T(256)(128)(2,1)} %param.25) | copy-start | bytes 772
  37.9 35.5 %copy-start.1 = (s32[256]{0:T(256)S(1)}, s32[256]{0:T(256)}, u32[]{:S(2)}) copy-start(s32[256]{0:T(256)} %param.22) | copy-start | bytes 3076
  37.9 36.2 %copy-start.2 = (s32[256]{0:T(256)S(1)}, s32[256]{0:T(256)}, u32[]{:S(2)}) copy-start(s32[256]{0:T(256)} %param.21) | copy-start | bytes 3076
  57.2 0.9 copy-start.3
  57.2 17.5 %copy-start.13 = (bf16[256]{0:T(256)(128)(2,1)S(1)}, bf16[256]{0:T(256)(128)(2,1)}, u32[]{:S(2)}) copy-start(bf16[256]{0:T(256)(128)(2,1)} %param.28) | copy-start | bytes 1540
  59.3 130.0 %all-gather.5.cloned.1.call-start = ((), (), s32[]{:S(2)}) async-start(), calls=%async_computation.8 | async-start | bytes 3932160 | tf_op jit(solution)/shard_map/all_gather | solution.py:20
  73.3 324.7 %reduce-scatter.2.cloned.1.call-start = ((), (), s32[]{:S(2)}) async-start(), calls=%async_computation.9 | async-start | bytes 7077888 | tf_op jit(solution)/shard_map/reduce_scatter | solution.py:165
  149.8 0.8 copy-start.6
  172.6 21.2 %copy-start.8 = (f32[1536]{0:T(1024)S(1)}, f32[1536]{0:T(1024)}, u32[]{:S(2)}) copy-start(f32[1536]{0:T(1024)} %param.30) | copy-start | bytes 18436
  192.6 1.1 copy-start.5
  272.9 9.5 %copy-start.11 = (bf16[1536,1120]{0,1:T(8,128)(2,1)S(1)}, bf16[1536,1120]{0,1:T(8,128)(2,1)}, u32[]{:S(2)}) copy-start(bf16[1536,1120]{0,1:T(8,128)(2,1)} %param.31) | copy-start | bytes 10321924
  301.4 99.6 %copy-start.9 = (f32[1536]{0:T(1024)S(1)}, f32[1536]{0:T(1024)}, u32[]{:S(2)}) copy-start(f32[1536]{0:T(1024)} %param.35) | copy-start | bytes 18436
  301.4 99.6 %copy-start.10 = (f32[1536]{0:T(1024)S(1)}, f32[1536]{0:T(1024)}, u32[]{:S(2)}) copy-start(f32[1536]{0:T(1024)} %param.34) | copy-start | bytes 18436
  399.7 0.9 copy-start.4
  410.9 14.3 %all-to-all-start.5 = ((f32[16,1,32]{2,1,0:T(1,128)}), f32[16,1,32]{2,1,0:T(1,128)S(1)}, u32[]{:S(2)}, u32[]{:S(2)}) async-start(f32[16,1,32]{2,1,0:T(1,128)} %broadcast_in_dim.31), calls=%async_computation.6 | async-start | bytes 16384 | tf_op jit(solution)/shard_map/all_to_all | solution.py:26
Sparse Core Ops, SparseCore 0:
  59.4 84.5 all-gather.2
  145.6 43.6 all-gather.4
  301.5 96.3 reduce-scatter.1
